TPU v7x, 128 devices: a whole 4x4x4 slice. The times are simulated.
128 devices in a mesh: expert: 16 (over x_hi, y, core), row: 8 (over z, x_lo).
Axes of the slice: x: 4 (x_hi: 2, x_lo: 2; x = x_hi * 2 + x_lo), y: 4, z: 4, core: 2. Of those that a mesh axis runs over, the one named last changes fastest.
Arguments:
- weights: bfloat16 [16, 7168, 2048], P('expert', 'row'), may hold values from -6 to 6
- left_bits: int32 [16, 7168], P('expert', 'row'), may hold values from 0 to 1
- right_bits: int32 [16, 2048], P('expert'), may hold values from 0 to 1
- groups: int32 [16, 2048], P('expert'), may hold values from 0 to 15, never falling along the last dimension, each value on 1 to 256 neighbouring positions
Outputs:
- scaled: bfloat16 [16, 7168, 2048], P('expert', 'row')
- block_error: float32 [16, 7168, 256], P('expert', 'row')
- scales: float32 [16, 16], P('expert')
- expert_error: float32 [16], P('expert')
- total_error: float32 [], replicated
Inputs may be any that keep to these rules, and one draw needn't show every extreme that they name: Along each expert's 2048 columns the group number never falls; each of the 16 groups holds 1 to 256 columns.
All inputs are finite; a program needn't handle non-finite values.
Results may differ from a plain program's by a relative error of at most 0.0091.
Values may be sent and summed in bfloat16 or wider, within the bound.
A program may use at most 128 MiB of HBM per device.

v0:
```python
import math
import jax
import jax.numpy as jnp
from jax import lax
from jax.sharding import PartitionSpec as P

D = 7168
FF = 2048
HB = 128
OUTER = 16
GROUPS = 16
BLOCKS = 56


def from_everyone(value, axis):
    peers = lax.axis_size(axis)
    return lax.all_to_all(
        jnp.broadcast_to(value[None], (peers, *value.shape)), axis, 0, 0, tiled=True
    )


def over_copies(value, axis):
    everything = from_everyone(value, axis)
    return jnp.max(everything, axis=0)


def taken_together(value, axis):
    return from_everyone(value, axis).sum(axis=0)


def sylvester(order):
    row_index = jnp.arange(order, dtype=jnp.int32)[:, None]
    col_index = jnp.arange(order, dtype=jnp.int32)[None, :]
    common = jnp.bitwise_and(row_index, col_index)
    parity = jnp.zeros((order, order), jnp.int32)
    for bit_pos in range(order.bit_length() - 1):
        parity = parity + jnp.bitwise_and(jnp.right_shift(common, bit_pos), 1)
    return (1 - 2 * jnp.bitwise_and(parity, 1)).astype(jnp.float32)


def cosine_block(order):
    first = jnp.arange(order, dtype=jnp.float32)[:, None]
    second = jnp.arange(order, dtype=jnp.float32)[None, :]
    table = math.sqrt(2.0 / order) * jnp.cos(math.pi * (2.0 * second + 1.0) * first / (2.0 * order))
    return jnp.where(first == 0.0, table * math.sqrt(0.5), table)


def coset_error(values):
    nearest = jnp.floor(values + 0.5)
    offset = values - nearest
    squares = jnp.sum(offset * offset, axis=-1)
    largest = jnp.max(jnp.abs(offset), axis=-1)
    parity = jnp.mod(jnp.sum(nearest, axis=-1), 2.0)
    return jnp.where(parity > 0.5, squares + 1.0 - 2.0 * largest, squares)


def lattice_error(values):
    octets = values.reshape(values.shape[:-1] + (values.shape[-1] // 8, 8))
    return jnp.minimum(coset_error(octets), coset_error(octets - 0.5))


def row_transform(mixed_rows, row_hadamard):
    turned = jnp.einsum("eibf,bk->eikf", mixed_rows, row_hadamard, precision=lax.Precision.HIGHEST)
    return turned / math.sqrt(HB)


def weight_of_rows(first_row, count):
    positions = (first_row + jnp.arange(count, dtype=jnp.int32)).astype(jnp.float32)
    return (1.0 + 4.0 * (positions + 0.5) / D) / 3.0


def group_scale(rotated, group_cols):
    column_peak = jnp.max(jnp.abs(rotated), axis=1)
    group_ids = jnp.arange(GROUPS, dtype=jnp.int32)
    in_group = group_cols[:, None, :] == group_ids[None, :, None]
    partial_peak = jnp.max(jnp.where(in_group, column_peak[:, None, :], 0.0), axis=2)
    group_peak = jnp.maximum(over_copies(partial_peak, "row"), 1.0)
    column_scale = jnp.sum(jnp.where(in_group, (2.0 / group_peak)[:, :, None], 0.0), axis=1)
    return (group_peak, column_scale)


def body(weights, left_bits, right_bits, groups):
    experts, local_rows, width = weights.shape
    blocks_here = local_rows // HB
    column_hadamard = sylvester(width // OUTER).astype(jnp.bfloat16)
    outer_hadamard = sylvester(OUTER)
    row_hadamard = sylvester(HB)
    block_matrix = cosine_block(BLOCKS).astype(jnp.bfloat16)
    left_sign = (2 * left_bits - 1).astype(jnp.float32)
    right_sign = (2 * right_bits - 1).astype(jnp.float32)
    signed = (weights.astype(jnp.float32) * left_sign[:, :, None] * right_sign[:, None, :]).astype(
        jnp.bfloat16
    )
    shaped = signed.reshape(experts, local_rows, OUTER, width // OUTER)
    inner = jnp.einsum("erpq,qs->erps", shaped, column_hadamard, preferred_element_type=jnp.float32)
    outer = jnp.einsum("erps,pt->erts", inner, outer_hadamard, precision=lax.Precision.HIGHEST)
    columns = (outer.reshape(experts, local_rows, width) / math.sqrt(FF)).astype(jnp.bfloat16)
    blocked = columns.reshape(experts, blocks_here, HB, width)
    column_slab = lax.all_to_all(blocked, "row", split_axis=3, concat_axis=1, tiled=True)
    mixed_rows = jnp.einsum(
        "ij,ejbf->eibf", block_matrix, column_slab, preferred_element_type=jnp.float32
    )
    turned = row_transform(mixed_rows, row_hadamard)
    rotated = lax.all_to_all(
        turned.astype(jnp.bfloat16), "row", split_axis=1, concat_axis=3, tiled=True
    ).astype(turned.dtype)
    rotated = rotated.reshape(experts, local_rows, width)
    group_peak, column_scale = group_scale(rotated, groups)
    values = rotated * column_scale[:, None, :]
    block_errors = lattice_error(values)
    row_weight = weight_of_rows(lax.axis_index("row") * local_rows, local_rows)
    partial_error = jnp.sum(block_errors * row_weight[None, :, None], axis=(1, 2)) / (D * FF // 8)
    scaled = values.astype(jnp.bfloat16)
    expert_count = experts * lax.axis_size("expert")
    expert_error = taken_together(partial_error, "row")
    total_error = taken_together(jnp.sum(expert_error), "expert") / expert_count
    return (scaled, block_errors, group_peak / 2.0, expert_error, total_error)


def solution(mesh):
    placed = (P("expert", "row", None), P("expert", "row"), P("expert", None), P("expert", None))
    return jax.shard_map(
        body,
        mesh=mesh,
        in_specs=placed,
        out_specs=(
            P("expert", "row", None),
            P("expert", "row", None),
            P("expert", None),
            P("expert"),
            P(),
        ),
        check_vma=False,
    )
```

profile of v0, /device:TPU:1, one launch (start us, length us, event | category | flops | bytes accessed | tf_op | source)
XLA Modules:
  0.0 254.1 jit_solution(4140201884117918043)
XLA Ops:
  0.6 0.7 add_convert_fusion
  1.3 0.7 convert_reduce_fusion
  2.0 3.1 %fusion.4 = bf16[112,8,16,128]{3,1,2,0:T(8,128)(2,1)S(1)} fusion(bf16[1,896,2048]{2,1,0:T(8,128)(2,1)} %param.4, f32[2048]{0:T(1024)S(1)} %bitcast.116, f32[896]{0:T(1024)S(1)} %convert_reduce_fusion), kind=kLoop, calls=%fused_computation.16 | loop fusion | flops 7340032 | bytes 7351808
  5.1 1.2 copy.61
  6.3 1.1 fusion.24
  7.5 8.3 %fusion.5 = bf16[1,896,16,128]{3,2,1,0:T(8,128)(2,1)} fusion(f32[896,16,128]{2,1,0:T(8,128)S(1)} %fusion.24), kind=kOutput, calls=%fused_computation.17 | convolution fusion | flops 355995648 | bytes 11010048 | tf_op jit(solution)/shard_map/erps,pt->erts/dot_general | solution.py:96
  15.8 6.7 %convert_element_type.172 = bf16[1,7,128,2048]{3,2,1,0:T(8,128)(2,1)} reshape(bf16[1,896,16,128]{3,2,1,0:T(8,128)(2,1)} %fusion.5) | data formatting | bytes 7340032 | tf_op jit(solution)/shard_map/convert_element_type | solution.py:97
  22.5 6.5 %copy.44 = bf16[1,7,128,2048]{2,1,0,3:T(8,128)(2,1)} copy(bf16[1,7,128,2048]{3,2,1,0:T(8,128)(2,1)} %convert_element_type.172) | data formatting | bytes 7340032 | tf_op jit(solution)/shard_map/convert_element_type | solution.py:97
  29.0 6.8 %all-to-all-start = ((bf16[1,7,128,2048]{2,1,0,3:T(8,128)(2,1)}), bf16[1,7,128,2048]{2,1,0,3:T(8,128)(2,1)}, u32[]{:S(2)}, u32[]{:S(2)}) async-start(bf16[1,7,128,2048]{2,1,0,3:T(8,128)(2,1)} %copy.44), calls=%async_computation | async-start | bytes 8388608 | tf_op jit(solution)/shard_map/all_to_all | solution.py:99
  35.8 48.7 %all-to-all-done = bf16[1,7,128,2048]{2,1,0,3:T(8,128)(2,1)} async-done(((bf16[1,7,128,2048]{2,1,0,3:T(8,128)(2,1)}), bf16[1,7,128,2048]{2,1,0,3:T(8,128)(2,1)}, u32[]{:S(2)}, u32[]{:S(2)}) %all-to-all-start) | async-done | bytes 3670048 | tf_op jit(solution)/shard_map/all_to_all | solution.py:99
  84.5 4.5 %copy.45 = bf16[1,7,128,2048]{2,3,1,0:T(8,128)(2,1)} copy(bf16[1,7,128,2048]{2,1,0,3:T(8,128)(2,1)} %all-to-all-done) | data formatting | bytes 7340032 | tf_op jit(solution)/shard_map/all_to_all | solution.py:99
  89.0 6.3 %copy.46 = bf16[1,8,7,128,256]{4,3,2,1,0:T(8,128)(2,1)} copy(bf16[1,8,7,128,256]{3,4,1,2,0:T(8,128)(2,1)} %bitcast.110) | data formatting | bytes 7340032 | tf_op jit(solution)/shard_map/all_to_all | solution.py:99
  95.3 5.1 %fusion.9 = f32[56,128,256]{2,0,1:T(8,128)S(1)} fusion(bf16[56,128,256]{2,1,0:T(8,128)(2,1)} %bitcast.109, f32[56]{0:T(128)S(1)} %add_multiply_fusion.1, pred[56]{0:T(512)(128)(4,1)S(1)} %iota_compare_fusion.1), kind=kOutput, calls=%fused_computation.21 | convolution fusion | flops 205539712 | bytes 11010328 | tf_op jit(solution)/shard_map/ij,ejbf->eibf/dot_general | solution.py:100
  100.4 9.8 %fusion.6 = bf16[1,56,128,256]{3,2,0,1:T(8,128)(2,1)} fusion(f32[56,128,256]{2,0,1:T(8,128)S(1)} %fusion.9), kind=kOutput, calls=%fused_computation.18 | convolution fusion | flops 2822651904 | bytes 11010048 | tf_op jit(solution)/shard_map/eibf,bk->eikf/dot_general | solution.py:63
  110.2 4.7 %all-to-all-start.1 = ((bf16[1,56,128,256]{3,2,0,1:T(8,128)(2,1)}), bf16[1,56,128,256]{3,2,0,1:T(8,128)(2,1)}, u32[]{:S(2)}, u32[]{:S(2)}) async-start(bf16[1,56,128,256]{3,2,0,1:T(8,128)(2,1)} %fusion.6), calls=%async_computation.1 | async-start | bytes 7340032 | tf_op jit(solution)/shard_map/all_to_all | solution.py:104
  114.9 42.1 %all-to-all-done.1 = bf16[1,56,128,256]{3,2,0,1:T(8,128)(2,1)} async-done(((bf16[1,56,128,256]{3,2,0,1:T(8,128)(2,1)}), bf16[1,56,128,256]{3,2,0,1:T(8,128)(2,1)}, u32[]{:S(2)}, u32[]{:S(2)}) %all-to-all-start.1) | async-done | bytes 3670048 | tf_op jit(solution)/shard_map/all_to_all | solution.py:104
  157.0 3.2 %abs_reduce_fusion.2 = f32[56,256]{1,0:T(8,128)S(1)} fusion(bf16[1,56,128,256]{3,2,0,1:T(8,128)(2,1)} %all-to-all-done.1), kind=kLoop, calls=%fused_computation.11 | loop fusion | flops 5490688 | bytes 3727360 | tf_op jit(solution)/shard_map/reduce_max | solution.py:73
  161.0 4.6 %all-to-all-start.2 = ((f32[8,1,16]{2,1,0:T(1,128)}), f32[8,1,16]{2,1,0:T(1,128)S(1)}, u32[]{:S(2)}, u32[]{:S(2)}) async-start(f32[8,1,16]{2,1,0:T(1,128)} %broadcast_in_dim.42), calls=%async_computation.2 | async-start | bytes 8192 | tf_op jit(solution)/shard_map/all_to_all | solution.py:17
  165.5 7.0 %copy.50 = f32[1,8,7,128,256]{3,2,4,1,0:T(8,128)} copy(bf16[1,8,7,128,256]{4,3,2,1,0:T(8,128)(2,1)} %bitcast.95) | data formatting | bytes 11010048 | tf_op jit(solution)/shard_map/convert_element_type | solution.py:106
  172.6 9.2 %reshape.657 = f32[1,896,256,8]{1,3,2,0:T(8,128)} reshape(f32[1,7,128,8,256]{2,1,4,3,0:T(8,128)} %bitcast.107) | data formatting | bytes 14680064 | tf_op jit(solution)/shard_map/convert_element_type | solution.py:106
  181.8 9.3 %reshape.664 = f32[1,896,2048]{1,2,0:T(8,128)} reshape(f32[1,7,128,8,256]{2,1,4,3,0:T(8,128)} %bitcast.108) | data formatting | bytes 14680064 | tf_op jit(solution)/shard_map/convert_element_type | solution.py:106
  191.1 8.6 %copy.58 = f32[1,896,2048]{2,1,0:T(8,128)} copy(f32[1,896,2048]{1,2,0:T(8,128)} %reshape.664) | data formatting | bytes 14680064 | tf_op jit(solution)/shard_map/convert_element_type | solution.py:106
  200.4 19.5 %fusion.3 = (f32[896,256]{0,1:T(8,128)S(1)}, f32[896,256]{0,1:T(8,128)S(1)}, f32[896,256]{0,1:T(8,128)S(1)}, f32[896,256]{0,1:T(8,128)S(1)}, f32[896,256]{0,1:T(8,128)S(1)}, /*index=5*/f32[896,256]{0,1:T(8,128)S(1)}) fusion(f32[1,896,256,8]{1,3,2,0:T(8,128)} %reshape.657, f32[256,8]{1,0:T(8,128)S(1)} %mul.272), kind=kLoop, calls=%fused_computation.9 | loop fusion | flops 29818880 | bytes 12853248 | tf_op jit(solution)/shard_map/reduce_sum | solution.py:53
  219.9 1.9 multiply_reduce_fusion.2
  223.1 5.1 %all-to-all-start.3 = ((f32[8,1,1]{2,1,0:T(1,128)}), f32[8,1,1]{2,1,0:T(1,128)S(1)}, u32[]{:S(2)}, u32[]{:S(2)}) async-start(f32[8,1,1]{2,1,0:T(1,128)} %broadcast_in_dim.44), calls=%async_computation.3 | async-start | bytes 8192 | tf_op jit(solution)/shard_map/all_to_all | solution.py:17
  228.2 5.9 %multiply_convert_fusion = bf16[1,896,2048]{2,1,0:T(8,128)(2,1)} fusion(f32[1,896,2048]{2,1,0:T(8,128)} %copy.58, f32[2048]{0:T(1024)S(1)} %select_reduce_fusion), kind=kLoop, calls=%fused_computation.10 | loop fusion | flops 3670016 | bytes 11018240 | tf_op jit(solution)/shard_map/convert_element_type | solution.py:113
  234.1 0.6 reduce_sum.90
  234.7 1.2 broadcast_in_dim.45
  236.0 8.7 %all-to-all-start.4 = ((f32[16,1,1]{2,1,0:T(1,128)}), f32[16,1,1]{2,1,0:T(1,128)S(1)}, u32[]{:S(2)}, u32[]{:S(2)}) async-start(f32[16,1,1]{2,1,0:T(1,128)} %broadcast_in_dim.45), calls=%async_computation.4 | async-start | bytes 16384 | tf_op jit(solution)/shard_map/all_to_all | solution.py:17
  244.7 1.2 copy.55
  245.9 5.8 %all-to-all-done.4 = f32[16,1,1]{2,1,0:T(1,128)S(1)} async-done(((f32[16,1,1]{2,1,0:T(1,128)}), f32[16,1,1]{2,1,0:T(1,128)S(1)}, u32[]{:S(2)}, u32[]{:S(2)}) %all-to-all-start.4) | async-done | bytes 96 | tf_op jit(solution)/shard_map/all_to_all | solution.py:17
  251.7 0.6 reduce_sum.92
  (17 shorter events, 2.1 us)
Async XLA Ops:
  29.0 55.5 %all-to-all-start = ((bf16[1,7,128,2048]{2,1,0,3:T(8,128)(2,1)}), bf16[1,7,128,2048]{2,1,0,3:T(8,128)(2,1)}, u32[]{:S(2)}, u32[]{:S(2)}) async-start(bf16[1,7,128,2048]{2,1,0,3:T(8,128)(2,1)} %copy.44), calls=%async_computation | async-start | bytes 8388608 | tf_op jit(solution)/shard_map/all_to_all | solution.py:99
  110.2 50.1 %copy-start = (s32[1,2048]{1,0:T(1,128)S(1)}, s32[1,2048]{1,0:T(1,128)}, u32[]{:S(2)}) copy-start(s32[1,2048]{1,0:T(1,128)} %param.7) | copy-start | bytes 24580
  110.2 46.8 %all-to-all-start.1 = ((bf16[1,56,128,256]{3,2,0,1:T(8,128)(2,1)}), bf16[1,56,128,256]{3,2,0,1:T(8,128)(2,1)}, u32[]{:S(2)}, u32[]{:S(2)}) async-start(bf16[1,56,128,256]{3,2,0,1:T(8,128)(2,1)} %fusion.6), calls=%async_computation.1 | async-start | bytes 7340032 | tf_op jit(solution)/shard_map/all_to_all | solution.py:104
  161.0 38.7 %all-to-all-start.2 = ((f32[8,1,16]{2,1,0:T(1,128)}), f32[8,1,16]{2,1,0:T(1,128)S(1)}, u32[]{:S(2)}, u32[]{:S(2)}) async-start(f32[8,1,16]{2,1,0:T(1,128)} %broadcast_in_dim.42), calls=%async_computation.2 | async-start | bytes 8192 | tf_op jit(solution)/shard_map/all_to_all | solution.py:17
  223.1 11.1 %all-to-all-start.3 = ((f32[8,1,1]{2,1,0:T(1,128)}), f32[8,1,1]{2,1,0:T(1,128)S(1)}, u32[]{:S(2)}, u32[]{:S(2)}) async-start(f32[8,1,1]{2,1,0:T(1,128)} %broadcast_in_dim.44), calls=%async_computation.3 | async-start | bytes 8192 | tf_op jit(solution)/shard_map/all_to_all | solution.py:17
  236.0 15.7 %all-to-all-start.4 = ((f32[16,1,1]{2,1,0:T(1,128)}), f32[16,1,1]{2,1,0:T(1,128)S(1)}, u32[]{:S(2)}, u32[]{:S(2)}) async-start(f32[16,1,1]{2,1,0:T(1,128)} %broadcast_in_dim.45), calls=%async_computation.4 | async-start | bytes 16384 | tf_op jit(solution)/shard_map/all_to_all | solution.py:17
where the time goes:
time: 256 us; the launch traced here: 254 us
  waiting for transfers between devices  96.6 us (38%)
  local copies, waits for them, and re-layouts  63.1 us (25%)
  other arithmetic  37 us (14%)
  starting transfers between devices  29.9 us (12%)
  matrix products  24.4 us (10%)
  between operations  3.17 us (1%)
    all_to_all x1, waiting for transfers between devices, body(): lax.all_to_all(blocked, 'row', split_axis=3, concat_axis=1, tiled=True)  48.7 us
    all_to_all x1, waiting for transfers between devices, body(): lax.all_to_all(turned.astype(jnp.bfloat16), 'row', split_axis=1, concat_a...  42.1 us
    convert_element_type x4, local copies, waits for them, and re-layouts, body(): rotated = lax.all_to_all(turned.astype(jnp.bfloat16), 'row', split_axis=1...  34.1 us
    reduce_sum x1, other arithmetic, coset_error(): parity = jnp.mod(jnp.sum(nearest, axis=-1), 2.0)  19.5 us
    all_to_all x3, starting transfers between devices, from_everyone(): lax.all_to_all(jnp.broadcast_to(value[None], (peers, *value.shape)), axis...  18.4 us
    convert_element_type x2, local copies, waits for them, and re-layouts, body(): (outer.reshape(experts, local_rows, width) / math.sqrt(FF)).astype(jnp.bf...  13.1 us
    all_to_all x2, local copies, waits for them, and re-layouts, body(): lax.all_to_all(blocked, 'row', split_axis=3, concat_axis=1, tiled=True)  10.8 us
    dot_general x1, matrix products, row_transform(): jnp.einsum('eibf,bk->eikf', mixed_rows, row_hadamard, precision=lax.Preci...  9.8 us
  transfers between devices with their start and end apart: 5, of which 3 were waited for; matrix products, arithmetic and copies ran while one was open for 16% of the time, Pallas kernels for 0%

commit v1 on v0

--- a/solution.py
+++ b/solution.py
@@ -96,7 +96,10 @@
     outer = jnp.einsum("erps,pt->erts", inner, outer_hadamard, precision=lax.Precision.HIGHEST)
     columns = (outer.reshape(experts, local_rows, width) / math.sqrt(FF)).astype(jnp.bfloat16)
     blocked = columns.reshape(experts, blocks_here, HB, width)
-    column_slab = lax.all_to_all(blocked, "row", split_axis=3, concat_axis=1, tiled=True)
+    column_slab = jnp.concatenate(
+        lax.all_to_all(jnp.stack(jnp.split(blocked, lax.axis_size("row"), axis=3)), "row", 0, 0),
+        axis=1,
+    )
     mixed_rows = jnp.einsum(
         "ij,ejbf->eibf", block_matrix, column_slab, preferred_element_type=jnp.float32
     )

time: 256 us -> 247 us (0.965)
  waiting for transfers between devices: 96.6 us -> 91 us
  local copies, waits for them, and re-layouts: 63.1 us -> 60.3 us
    unnamed x5 -> x12, local copies, waits for them, and re-layouts: 2.44 us -> 15.1 us
    all_to_all x2 -> x0, local copies, waits for them, and re-layouts: 10.8 us -> none  [body(): lax.all_to_all(blocked, 'row', split_axis=3, concat_axis=1, tiled=True)]
    convert_element_type x2 -> x1, local copies, waits for them, and re-layouts: 13.1 us -> 6.67 us  [body(): (outer.reshape(experts, local_rows, width) / math.sqrt(FF)).astype(jnp.bf...]
    all_to_all x1, waiting for transfers between devices: 48.7 us -> 43.1 us  [body(): lax.all_to_all(jnp.stack(jnp.split(blocked, lax.axis_size('row'), axis=3)...]
  transfers between devices with their start and end apart: 5 -> 5, of which waited for: 3 -> 3; matrix products, arithmetic and copies ran while one was open for 16% -> 17% of each run, Pallas kernels for 0% -> 0%
where the time goes in v1:
time: 247 us; the launch traced here: 246 us
  waiting for transfers between devices  91 us (37%)
  local copies, waits for them, and re-layouts  60.3 us (24%)
  other arithmetic  37 us (15%)
  starting transfers between devices  29.8 us (12%)
  matrix products  24.4 us (10%)
  between operations  3.18 us (1%)
    all_to_all x1, waiting for transfers between devices, body(): lax.all_to_all(jnp.stack(jnp.split(blocked, lax.axis_size('row'), axis=3)...  43.1 us
    all_to_all x1, waiting for transfers between devices, body(): lax.all_to_all(turned.astype(jnp.bfloat16), 'row', split_axis=1, concat_a...  42.1 us
    convert_element_type x4, local copies, waits for them, and re-layouts, body(): rotated = lax.all_to_all(turned.astype(jnp.bfloat16), 'row', split_axis=1...  34.1 us
    reduce_sum x1, other arithmetic, coset_error(): parity = jnp.mod(jnp.sum(nearest, axis=-1), 2.0)  19.5 us
    all_to_all x3, starting transfers between devices, from_everyone(): lax.all_to_all(jnp.broadcast_to(value[None], (peers, *value.shape)), axis...  18.4 us
    unnamed x12, local copies, waits for them, and re-layouts  15.1 us
    dot_general x1, matrix products, row_transform(): jnp.einsum('eibf,bk->eikf', mixed_rows, row_hadamard, precision=lax.Preci...  9.8 us
    dot_general x1, matrix products, body(): jnp.einsum('erps,pt->erts', inner, outer_hadamard, precision=lax.Precisio...  8.35 us
  transfers between devices with their start and end apart: 5, of which 3 were waited for; matrix products, arithmetic and copies ran while one was open for 17% of the time, Pallas kernels for 0%

profile of v1, /device:TPU:1, one launch (start us, length us, event | category | flops | bytes accessed | tf_op | source)
XLA Modules:
  0.0 245.6 jit_solution(8982546404757824021)
XLA Ops:
  2.0 3.1 %fusion.4 = bf16[112,8,16,128]{3,1,2,0:T(8,128)(2,1)S(1)} fusion(bf16[1,896,2048]{2,1,0:T(8,128)(2,1)} %param.4, f32[2048]{0:T(1024)S(1)} %bitcast.143, f32[896]{0:T(1024)S(1)} %convert_reduce_fusion), kind=kLoop, calls=%fused_computation.16 | loop fusion | flops 7340032 | bytes 7351808
  5.1 1.2 copy.52
  7.5 8.3 %fusion.5 = bf16[1,896,16,128]{3,2,1,0:T(8,128)(2,1)} fusion(f32[896,16,128]{2,1,0:T(8,128)S(1)} %fusion.32), kind=kOutput, calls=%fused_computation.17 | convolution fusion | flops 355995648 | bytes 11010048 | tf_op jit(solution)/shard_map/erps,pt->erts/dot_general | solution.py:96
  15.8 6.7 %convert_element_type.172 = bf16[1,7,128,2048]{3,2,1,0:T(8,128)(2,1)} reshape(bf16[1,896,16,128]{3,2,1,0:T(8,128)(2,1)} %fusion.5) | data formatting | bytes 7340032 | tf_op jit(solution)/shard_map/convert_element_type | solution.py:97
  22.5 1.8 fusion.28
  24.3 1.8 fusion.27
  26.1 1.8 fusion.26
  27.9 1.8 fusion.25
  29.8 1.8 fusion.24
  31.6 1.8 fusion.23
  33.4 1.8 fusion.22
  35.2 1.8 fusion.21
  37.0 6.8 %all-to-all-start = ((bf16[8,1,7,128,256]{4,3,2,1,0:T(8,128)(2,1)}), bf16[8,1,7,128,256]{4,3,2,1,0:T(8,128)(2,1)}, u32[]{:S(2)}, u32[]{:S(2)}) async-start(bf16[8,1,7,128,256]{4,3,2,1,0:T(8,128)(2,1)} %fusion.21), calls=%async_computation | async-start | bytes 7340032 | tf_op jit(solution)/shard_map/all_to_all | solution.py:100
  43.8 43.1 %all-to-all-done = bf16[8,1,7,128,256]{4,3,2,1,0:T(8,128)(2,1)} async-done(((bf16[8,1,7,128,256]{4,3,2,1,0:T(8,128)(2,1)}), bf16[8,1,7,128,256]{4,3,2,1,0:T(8,128)(2,1)}, u32[]{:S(2)}, u32[]{:S(2)}) %all-to-all-start) | async-done | bytes 3670048 | tf_op jit(solution)/shard_map/all_to_all | solution.py:100
  86.9 5.1 %fusion.9 = f32[56,128,256]{2,0,1:T(8,128)S(1)} fusion(bf16[56,128,256]{2,1,0:T(8,128)(2,1)} %bitcast.14, f32[56]{0:T(128)S(1)} %add_multiply_fusion.1, pred[56]{0:T(512)(128)(4,1)S(1)} %iota_compare_fusion.1), kind=kOutput, calls=%fused_computation.21 | convolution fusion | flops 205539712 | bytes 11010328 | tf_op jit(solution)/shard_map/ij,ejbf->eibf/dot_general | solution.py:103
  92.0 9.8 %fusion.6 = bf16[1,56,128,256]{3,2,0,1:T(8,128)(2,1)} fusion(f32[56,128,256]{2,0,1:T(8,128)S(1)} %fusion.9), kind=kOutput, calls=%fused_computation.18 | convolution fusion | flops 2822651904 | bytes 11010048 | tf_op jit(solution)/shard_map/eibf,bk->eikf/dot_general | solution.py:63
  101.8 4.6 %all-to-all-start.1 = ((bf16[1,56,128,256]{3,2,0,1:T(8,128)(2,1)}), bf16[1,56,128,256]{3,2,0,1:T(8,128)(2,1)}, u32[]{:S(2)}, u32[]{:S(2)}) async-start(bf16[1,56,128,256]{3,2,0,1:T(8,128)(2,1)} %fusion.6), calls=%async_computation.1 | async-start | bytes 7340032 | tf_op jit(solution)/shard_map/all_to_all | solution.py:107
  106.3 42.1 %all-to-all-done.1 = bf16[1,56,128,256]{3,2,0,1:T(8,128)(2,1)} async-done(((bf16[1,56,128,256]{3,2,0,1:T(8,128)(2,1)}), bf16[1,56,128,256]{3,2,0,1:T(8,128)(2,1)}, u32[]{:S(2)}, u32[]{:S(2)}) %all-to-all-start.1) | async-done | bytes 3670048 | tf_op jit(solution)/shard_map/all_to_all | solution.py:107
  148.5 3.2 %abs_reduce_fusion.2 = f32[56,256]{1,0:T(8,128)S(1)} fusion(bf16[1,56,128,256]{3,2,0,1:T(8,128)(2,1)} %all-to-all-done.1), kind=kLoop, calls=%fused_computation.11 | loop fusion | flops 5490688 | bytes 3727360 | tf_op jit(solution)/shard_map/reduce_max | solution.py:73
  152.5 4.6 %all-to-all-start.2 = ((f32[8,1,16]{2,1,0:T(1,128)}), f32[8,1,16]{2,1,0:T(1,128)S(1)}, u32[]{:S(2)}, u32[]{:S(2)}) async-start(f32[8,1,16]{2,1,0:T(1,128)} %broadcast_in_dim.42), calls=%async_computation.2 | async-start | bytes 8192 | tf_op jit(solution)/shard_map/all_to_all | solution.py:17
  157.0 7.0 %copy.41 = f32[1,8,7,128,256]{3,2,4,1,0:T(8,128)} copy(bf16[1,8,7,128,256]{4,3,2,1,0:T(8,128)(2,1)} %bitcast.124) | data formatting | bytes 11010048 | tf_op jit(solution)/shard_map/convert_element_type | solution.py:109
  164.0 9.2 %reshape.658 = f32[1,896,256,8]{1,3,2,0:T(8,128)} reshape(f32[1,7,128,8,256]{2,1,4,3,0:T(8,128)} %bitcast.136) | data formatting | bytes 14680064 | tf_op jit(solution)/shard_map/convert_element_type | solution.py:109
  173.3 9.3 %reshape.665 = f32[1,896,2048]{1,2,0:T(8,128)} reshape(f32[1,7,128,8,256]{2,1,4,3,0:T(8,128)} %bitcast.137) | data formatting | bytes 14680064 | tf_op jit(solution)/shard_map/convert_element_type | solution.py:109
  182.5 8.6 %copy.49 = f32[1,896,2048]{2,1,0:T(8,128)} copy(f32[1,896,2048]{1,2,0:T(8,128)} %reshape.665) | data formatting | bytes 14680064 | tf_op jit(solution)/shard_map/convert_element_type | solution.py:109
  191.9 19.5 %fusion.3 = (f32[896,256]{0,1:T(8,128)S(1)}, f32[896,256]{0,1:T(8,128)S(1)}, f32[896,256]{0,1:T(8,128)S(1)}, f32[896,256]{0,1:T(8,128)S(1)}, f32[896,256]{0,1:T(8,128)S(1)}, /*index=5*/f32[896,256]{0,1:T(8,128)S(1)}) fusion(f32[1,896,256,8]{1,3,2,0:T(8,128)} %reshape.658, f32[256,8]{1,0:T(8,128)S(1)} %mul.272), kind=kLoop, calls=%fused_computation.9 | loop fusion | flops 29818880 | bytes 12853248 | tf_op jit(solution)/shard_map/reduce_sum | solution.py:53
  211.4 1.9 multiply_reduce_fusion.2
  214.5 5.1 %all-to-all-start.3 = ((f32[8,1,1]{2,1,0:T(1,128)}), f32[8,1,1]{2,1,0:T(1,128)S(1)}, u32[]{:S(2)}, u32[]{:S(2)}) async-start(f32[8,1,1]{2,1,0:T(1,128)} %broadcast_in_dim.44), calls=%async_computation.3 | async-start | bytes 8192 | tf_op jit(solution)/shard_map/all_to_all | solution.py:17
  219.7 5.9 %multiply_convert_fusion = bf16[1,896,2048]{2,1,0:T(8,128)(2,1)} fusion(f32[1,896,2048]{2,1,0:T(8,128)} %copy.49, f32[2048]{0:T(1024)S(1)} %select_reduce_fusion), kind=kLoop, calls=%fused_computation.10 | loop fusion | flops 3670016 | bytes 11018240 | tf_op jit(solution)/shard_map/convert_element_type | solution.py:116
  226.2 1.2 broadcast_in_dim.45
  227.4 8.7 %all-to-all-start.4 = ((f32[16,1,1]{2,1,0:T(1,128)}), f32[16,1,1]{2,1,0:T(1,128)S(1)}, u32[]{:S(2)}, u32[]{:S(2)}) async-start(f32[16,1,1]{2,1,0:T(1,128)} %broadcast_in_dim.45), calls=%async_computation.4 | async-start | bytes 16384 | tf_op jit(solution)/shard_map/all_to_all | solution.py:17
  236.2 1.2 copy.46
  237.4 5.8 %all-to-all-done.4 = f32[16,1,1]{2,1,0:T(1,128)S(1)} async-done(((f32[16,1,1]{2,1,0:T(1,128)}), f32[16,1,1]{2,1,0:T(1,128)S(1)}, u32[]{:S(2)}, u32[]{:S(2)}) %all-to-all-start.4) | async-done | bytes 96 | tf_op jit(solution)/shard_map/all_to_all | solution.py:17
  (22 shorter events, 5.9 us)
Async XLA Ops:
  37.0 49.9 %all-to-all-start = ((bf16[8,1,7,128,256]{4,3,2,1,0:T(8,128)(2,1)}), bf16[8,1,7,128,256]{4,3,2,1,0:T(8,128)(2,1)}, u32[]{:S(2)}, u32[]{:S(2)}) async-start(bf16[8,1,7,128,256]{4,3,2,1,0:T(8,128)(2,1)} %fusion.21), calls=%async_computation | async-start | bytes 7340032 | tf_op jit(solution)/shard_map/all_to_all | solution.py:100
  101.8 46.7 %all-to-all-start.1 = ((bf16[1,56,128,256]{3,2,0,1:T(8,128)(2,1)}), bf16[1,56,128,256]{3,2,0,1:T(8,128)(2,1)}, u32[]{:S(2)}, u32[]{:S(2)}) async-start(bf16[1,56,128,256]{3,2,0,1:T(8,128)(2,1)} %fusion.6), calls=%async_computation.1 | async-start | bytes 7340032 | tf_op jit(solution)/shard_map/all_to_all | solution.py:107
  106.3 45.4 %copy-start = (s32[1,2048]{1,0:T(1,128)S(1)}, s32[1,2048]{1,0:T(1,128)}, u32[]{:S(2)}) copy-start(s32[1,2048]{1,0:T(1,128)} %param.7) | copy-start | bytes 24580
  152.5 38.7 %all-to-all-start.2 = ((f32[8,1,16]{2,1,0:T(1,128)}), f32[8,1,16]{2,1,0:T(1,128)S(1)}, u32[]{:S(2)}, u32[]{:S(2)}) async-start(f32[8,1,16]{2,1,0:T(1,128)} %broadcast_in_dim.42), calls=%async_computation.2 | async-start | bytes 8192 | tf_op jit(solution)/shard_map/all_to_all | solution.py:17
  214.5 11.1 %all-to-all-start.3 = ((f32[8,1,1]{2,1,0:T(1,128)}), f32[8,1,1]{2,1,0:T(1,128)S(1)}, u32[]{:S(2)}, u32[]{:S(2)}) async-start(f32[8,1,1]{2,1,0:T(1,128)} %broadcast_in_dim.44), calls=%async_computation.3 | async-start | bytes 8192 | tf_op jit(solution)/shard_map/all_to_all | solution.py:17
  227.4 15.7 %all-to-all-start.4 = ((f32[16,1,1]{2,1,0:T(1,128)}), f32[16,1,1]{2,1,0:T(1,128)S(1)}, u32[]{:S(2)}, u32[]{:S(2)}) async-start(f32[16,1,1]{2,1,0:T(1,128)} %broadcast_in_dim.45), calls=%async_computation.4 | async-start | bytes 16384 | tf_op jit(solution)/shard_map/all_to_all | solution.py:17
